TPU v7x, 32 devices: a whole 2x2x4 slice. The times are simulated.
32 devices in a mesh: row: 4 (over z), col: 8 (over y, x, core).
Axes of the slice: x: 2, y: 2, z: 4, core: 2. Of those that a mesh axis runs over, the one named last changes fastest.
Arguments:
- ainv_anc: bfloat16 [12288, 12288], P('row', 'col'), may hold values from -6 to 6
- l_panel: bfloat16 [1536, 12288], P('col', 'row'), may hold values from -0.109375 to 0.109375
- diag_inv: float32 [1536, 768], P('col', 'row'), may hold values from -6 to 6
- struct_mask: int32 [2, 96], replicated, may hold values 0 or 1
- pieces: float32 [1536, 32, 128], P(('row', 'col')), may hold values from -6 to 6
- tile_owner: int32 [1536, 1], P(('row', 'col')), may hold values from 0 to 31; in each aligned block of 48 rows (0 to 47, 48 to 95, ...) at most 3 rows name the same one
Outputs:
- ainv_upper: bfloat16 [1536, 12288], P('col', 'row')
- ainv_diag: float32 [1536, 768], P('col', 'row')
- moved: float32 [3072, 32, 128], P(('row', 'col'))
Inputs may be any that keep to these rules, and one draw needn't show every extreme that they name: `tile_owner`: among the 48 pieces of one device no owner is named more than 3 times, a bound that some block reaches.
All inputs are finite; a program needn't handle non-finite values.
Results may differ from a plain program's by a relative error of at most 0.015.
Values may be sent and summed in bfloat16 or wider, within the bound.
A program may use at most 128 MiB of HBM per device.

v0:
```python
import jax
import jax.numpy as jnp
from jax import lax
from jax.sharding import PartitionSpec as P

W = 768
AB = 128
SLOT = 3


def broadcast(value, axis, root):
    mine = lax.axis_index(axis) == root
    return lax.psum(jnp.where(mine, value, jnp.zeros_like(value)), axis)


def local(ainv_anc, l_panel, diag_inv, struct_mask, pieces, tile_owner):
    row_devices = lax.axis_size("row")
    col_devices = lax.axis_size("col")
    row_index = lax.axis_index("row")
    col_index = lax.axis_index("col")
    slab_rows = l_panel.shape[0]
    local_rows = l_panel.shape[1]
    cross_width = ainv_anc.shape[1]
    group_ratio = col_devices // row_devices
    supernode = col_index * slab_rows // W
    block_count = local_rows // AB
    keep_blocks = lax.dynamic_slice(
        struct_mask, (supernode, row_index * block_count), (1, block_count)
    )
    keep_rows = (
        jnp.broadcast_to(keep_blocks[:, :, None], (1, block_count, AB)).reshape(1, local_rows) > 0
    )
    masked = jnp.where(keep_rows, l_panel, jnp.zeros_like(l_panel))
    gathered = lax.all_gather(masked, "col", axis=0, tiled=True)
    offset = col_index % group_ratio * cross_width
    own_cross = lax.dynamic_slice_in_dim(gathered, offset, cross_width, 1)
    cross_rows = broadcast(own_cross, "row", col_index // group_ratio)
    product = lax.psum_scatter(
        lax.dot_general(
            cross_rows, ainv_anc, (((1,), (1,)), ((), ())), preferred_element_type=jnp.float32
        ).astype(jnp.bfloat16),
        "col",
        scatter_dimension=0,
        tiled=True,
    ).astype(jnp.float32)
    upper_rows = jnp.where(keep_rows, -product, jnp.zeros_like(product)).astype(jnp.bfloat16)
    own_block = lax.dynamic_slice_in_dim(gathered, supernode * W, W, 0)
    diag_part = lax.dot_general(
        upper_rows, own_block, (((1,), (1,)), ((), ())), preferred_element_type=jnp.float32
    )
    summed = lax.psum_scatter(
        diag_part.astype(jnp.bfloat16), "row", scatter_dimension=1, tiled=True
    ).astype(jnp.float32)
    ainv_diag = diag_inv - summed
    devices_all = row_devices * col_devices
    owners = tile_owner[:, 0]
    onehot = (owners[:, None] == jnp.arange(devices_all, dtype=jnp.int32)[None, :]).astype(
        jnp.int32
    )
    earlier = jnp.cumsum(onehot, axis=0) - onehot
    rank_in_dest = jnp.sum(earlier * onehot, axis=1)
    slot_index = owners * SLOT + rank_in_dest
    piece_rows = pieces.shape[1]
    piece_cols = pieces.shape[2]
    buffer = (
        jnp.zeros((devices_all * SLOT, piece_rows, piece_cols), jnp.float32)
        .at[slot_index]
        .set(pieces)
    )
    shaped = buffer.reshape(devices_all, SLOT, piece_rows, piece_cols)
    arrived = lax.all_to_all(
        shaped.astype(jnp.bfloat16), ("row", "col"), split_axis=0, concat_axis=0, tiled=True
    ).astype(shaped.dtype)
    moved_pieces = arrived.reshape(devices_all * SLOT, piece_rows, piece_cols)
    return (upper_rows, ainv_diag, moved_pieces)


def solution(mesh):
    in_specs = (
        P("row", "col"),
        P("col", "row"),
        P("col", "row"),
        P(),
        P(("row", "col"), None, None),
        P(("row", "col"), None),
    )
    out_specs = (P("col", "row"), P("col", "row"), P(("row", "col"), None, None))
    return jax.shard_map(local, mesh=mesh, in_specs=in_specs, out_specs=out_specs, check_vma=False)
```

profile of v0, /device:TPU:0, one launch (start us, length us, event | category | flops | bytes accessed | tf_op | source)
XLA Modules:
  0.0 382.2 jit_solution(5946898883278234848)
XLA Ops:
  7.2 0.8 compare_bitcast_fusion
  8.0 0.1 broadcast_bitcast_fusion
  8.1 2.4 broadcast_select_fusion
  10.5 0.0 all-reduce.2.cloned.1.call-start
  10.6 61.5 %all-gather.2.cloned.1.call-done = bf16[1536,3072]{1,0:T(8,128)(2,1)} async-done(((bf16[192,3072]{1,0:T(8,128)(2,1)}), bf16[1536,3072]{1,0:T(8,128)(2,1)}) %all-gather.2.cloned.1.call-update) | async-done | bytes 9437200 | tf_op jit(solution)/shard_map/all_gather | solution.py:34
  72.1 5.4 %dynamic-slice_select_fusion = bf16[1536,1536]{1,0:T(8,128)(2,1)} fusion(bf16[1536,3072]{1,0:T(8,128)(2,1)} %all-gather.2.cloned.1.call-done, s32[]{:T(128)S(6)} %select_n.53, pred[]{:T(512)S(6)} %eq.20), kind=kLoop, calls=%fused_computation.4 | loop fusion | flops 2359296 | bytes 9437189 | tf_op jit(solution)/shard_map/jit(_where)/select_n | solution.py:13
  77.5 172.1 %all-reduce.2.cloned.1.call-done = bf16[1536,1536]{1,0:T(8,128)(2,1)} async-done(((bf16[1536,1536]{1,0:T(8,128)(2,1)}), bf16[1536,1536]{1,0:T(8,128)(2,1)}) %all-reduce.2.cloned.1.call-update) | async-done | bytes 4718608 | tf_op jit(solution)/shard_map/psum | solution.py:13
  249.6 20.5 %convolution_convert_fusion = bf16[1536,3072]{1,0:T(8,128)(2,1)} fusion(bf16[1536,1536]{1,0:T(8,128)(2,1)} %all-reduce.2.cloned.1.call-done, bf16[3072,1536]{1,0:T(8,128)(2,1)} %param.6), kind=kOutput, calls=%fused_computation.1 | convolution fusion | flops 14500233216 | bytes 23592960 | tf_op jit(solution)/shard_map/dot_general | solution.py:39
  270.1 0.6 copy-done.3
  270.7 0.1 fusion.5
  270.8 0.1 reduce_window_sum.11
  270.9 0.2 select_reduce_fusion
  271.1 0.2 broadcast_in_dim.39
  271.3 2.0 scatter_fusion
  273.3 1.0 convert_element_type.31
  274.3 3.6 all-to-all-start
  277.9 68.1 %reduce-scatter.5.cloned.1.call-done = bf16[192,3072]{1,0:T(8,128)(2,1)} async-done(((bf16[1536,3072]{1,0:T(8,128)(2,1)}), bf16[192,3072]{1,0:T(8,128)(2,1)}) %reduce-scatter.5.cloned.1.call-update) | async-done | bytes 1179664 | tf_op jit(solution)/shard_map/reduce_scatter | solution.py:38
  346.0 1.6 select_convert_fusion
  347.6 4.5 %fusion.2 = bf16[192,768]{1,0:T(8,128)(2,1)S(1)} fusion(bf16[192,3072]{1,0:T(8,128)(2,1)S(1)} %select_convert_fusion, bf16[1536,3072]{1,0:T(8,128)(2,1)} %all-gather.2.cloned.1.call-done, s32[]{:T(128)S(6)} %select_n.56), kind=kOutput, calls=%fused_computation.6 | convolution fusion | flops 906117120 | bytes 6193156 | tf_op jit(solution)/shard_map/dot_general | solution.py:48
  352.1 0.9 copy.9
  353.1 1.4 bitcast_convert_fusion
  354.5 19.5 %reduce-scatter.7.cloned.1.call-done = bf16[192,192]{1,0:T(8,128)(2,1)} async-done(((bf16[768,192]{1,0:T(8,128)(2,1)}), bf16[192,192]{1,0:T(8,128)(2,1)}) %reduce-scatter.7.cloned.1.call-update) | async-done | bytes 73744
  374.0 1.0 copy.10
  375.0 0.7 convert_subtract_fusion
  (16 shorter events, 0.2 us)
Async XLA Ops:
  7.2 64.9 %all-gather.2.cloned.1.call-start = ((), (), s32[]{:S(2)}) async-start(), calls=%async_computation.3 | async-start | bytes 10616832 | tf_op jit(solution)/shard_map/all_gather | solution.py:34
  10.5 239.1 %all-reduce.2.cloned.1.call-start = ((), (), s32[]{:S(2)}) async-start(), calls=%async_computation.4 | async-start | bytes 9437184 | tf_op jit(solution)/shard_map/psum | solution.py:13
  77.5 268.6 %reduce-scatter.5.cloned.1.call-start = ((), (), s32[]{:S(2)}) async-start(), calls=%async_computation.5 | async-start | bytes 10616832 | tf_op jit(solution)/shard_map/reduce_scatter | solution.py:38
  270.1 0.7 copy-start.3
  270.1 1.2 copy-start.1
  274.3 78.7 %all-to-all-start = ((bf16[32,3,32,128]{3,2,1,0:T(8,128)(2,1)}), bf16[32,3,32,128]{3,2,1,0:T(8,128)(2,1)S(1)}, u32[]{:S(2)}, u32[]{:S(2)}) async-start(bf16[32,3,32,128]{3,2,1,0:T(8,128)(2,1)} %bitcast.5), calls=%async_computation.1 | async-start | bytes 1572864 | tf_op jit(solution)/shard_map/all_to_all | solution.py:71
  277.9 96.1 %reduce-scatter.7.cloned.1.call-start = ((), (), s32[]{:S(2)}) async-start(), calls=%async_computation.6 | async-start | bytes 491520
  347.6 4.5 %copy-start = (bf16[192,3072]{1,0:T(8,128)(2,1)}, bf16[192,3072]{1,0:T(8,128)(2,1)S(1)}, u32[]{:S(2)}) copy-start(bf16[192,3072]{1,0:T(8,128)(2,1)S(1)} %select_convert_fusion) | copy-start | bytes 3538948
  352.1 22.9 %copy-start.2 = (f32[192,192]{1,0:T(8,128)S(1)}, f32[192,192]{1,0:T(8,128)}, u32[]{:S(2)}) copy-start(f32[192,192]{1,0:T(8,128)} %param.8) | copy-start | bytes 442372
Sparse Core Ops, SparseCore 0:
  10.6 61.4 all-gather.1
  77.6 171.9 all-reduce.1
  270.2 75.7 reduce-scatter.4
  353.2 20.7 reduce-scatter.6
where the time goes:
time: 383 us; the launch traced here: 382 us
  waiting for transfers between devices  321 us (84%)
  matrix products  25 us (7%)
  between operations  13.9 us (4%)
  other arithmetic  13.6 us (4%)
  local copies, waits for them, and re-layouts  4.82 us (1%)
    psum x1, waiting for transfers between devices, broadcast(): return lax.psum(jnp.where(mine, value, jnp.zeros_like(value)), axis)  172 us
    reduce_scatter x1, waiting for transfers between devices, local(): lax.psum_scatter(lax.dot_general(cross_rows, ainv_anc, (((1,), (1,)), (()...  68.1 us
    all_gather x1, waiting for transfers between devices, local(): gathered = lax.all_gather(masked, 'col', axis=0, tiled=True)  61.5 us
    dot_general x1, matrix products, local(): lax.dot_general(cross_rows, ainv_anc, (((1,), (1,)), ((), ())), preferred...  20.5 us
    unnamed x5, waiting for transfers between devices  19.6 us
  transfers between devices with their start and end apart: 5, of which 4 were waited for; matrix products, arithmetic and copies ran while one was open for 3% of the time, Pallas kernels for 0%

commit v1 on v0

--- a/solution.py
+++ b/solution.py
@@ -1,3 +1,4 @@
+import functools
 import jax
 import jax.numpy as jnp
 from jax import lax
@@ -6,6 +7,23 @@
 W = 768
 AB = 128
 SLOT = 3
+
+
+def edit_views(slab_in, bus_axis):
+    p_count = lax.axis_size(bus_axis)
+    local_now = sorted(((to_i, (to_i + 1) % p_count) for to_i in range(p_count)))
+    response = slab_in
+    crops = [response]
+    for m in range(1, p_count):
+        response = lax.ppermute(response, bus_axis, local_now)
+        crops.insert(0, response)
+    outcome_arr = jnp.concatenate(crops, axis=0)
+    now = lax.axis_index(bus_axis) + 1
+    parts_out = jnp.roll(outcome_arr, now * slab_in.shape[0], axis=0)
+    return parts_out
+
+
+direct_stages_all_in = functools.partial(edit_views, bus_axis="col")
 
 
 def broadcast(value, axis, root):
@@ -31,7 +49,7 @@
         jnp.broadcast_to(keep_blocks[:, :, None], (1, block_count, AB)).reshape(1, local_rows) > 0
     )
     masked = jnp.where(keep_rows, l_panel, jnp.zeros_like(l_panel))
-    gathered = lax.all_gather(masked, "col", axis=0, tiled=True)
+    gathered = direct_stages_all_in(masked)
     offset = col_index % group_ratio * cross_width
     own_cross = lax.dynamic_slice_in_dim(gathered, offset, cross_width, 1)
     cross_rows = broadcast(own_cross, "row", col_index // group_ratio)

time: 383 us -> 454 us (1.19)
  waiting for transfers between devices: 321 us -> 377 us
  local copies, waits for them, and re-layouts: 4.82 us -> 20.4 us
    ppermute x0 -> x7, waiting for transfers between devices: none -> 116 us  [edit_views(): response = lax.ppermute(response, bus_axis, local_now)]
    all_gather x1 -> x0, waiting for transfers between devices: 61.5 us -> none  [local(): gathered = lax.all_gather(masked, 'col', axis=0, tiled=True)]
    unnamed x10 -> x36, local copies, waits for them, and re-layouts: 2.55 us -> 18.1 us
    unnamed x5 -> x4, waiting for transfers between devices: 19.6 us -> 19.6 us
  transfers between devices with their start and end apart: 5 -> 11, of which waited for: 4 -> 10; matrix products, arithmetic and copies ran while one was open for 3% -> 3% of each run, Pallas kernels for 0% -> 0%
where the time goes in v1:
time: 454 us
  waiting for transfers between devices  377 us (83%)
  matrix products  25.1 us (6%)
  local copies, waits for them, and re-layouts  20.4 us (4%)
  between operations  14 us (3%)
  other arithmetic  12.8 us (3%)
    psum x1, waiting for transfers between devices, broadcast(): return lax.psum(jnp.where(mine, value, jnp.zeros_like(value)), axis)  173 us
    ppermute x7, waiting for transfers between devices, edit_views(): response = lax.ppermute(response, bus_axis, local_now)  116 us
    reduce_scatter x1, waiting for transfers between devices, local(): lax.psum_scatter(lax.dot_general(cross_rows, ainv_anc, (((1,), (1,)), (()...  68.1 us
    dot_general x1, matrix products, local(): lax.dot_general(cross_rows, ainv_anc, (((1,), (1,)), ((), ())), preferred...  20.5 us
    unnamed x4, waiting for transfers between devices  19.6 us
    unnamed x36, local copies, waits for them, and re-layouts  18.1 us
  transfers between devices with their start and end apart: 11, of which 10 were waited for; matrix products, arithmetic and copies ran while one was open for 3% of the time, Pallas kernels for 0%

profile of v1, /device:TPU:0, one launch (start us, length us, event | category | flops | bytes accessed | tf_op | source)
XLA Modules:
  0.0 453.7 jit_solution(5319764674192437781)
XLA Ops:
  8.1 1.4 broadcast_select_fusion
  10.0 16.8 %collective-permute-done = bf16[192,3072]{1,0:T(8,128)(2,1)S(1)} collective-permute-done((bf16[192,3072]{1,0:T(8,128)(2,1)S(1)}, bf16[192,3072]{1,0:T(8,128)(2,1)S(1)}, u32[]{:S(2)}, u32[]{:S(2)}) %collective-permute-start) | collective-permute-done | bytes 1179680 | tf_op jit(solution)/shard_map/ppermute | solution.py:18
  26.7 16.5 %collective-permute-done.1 = bf16[192,3072]{1,0:T(8,128)(2,1)S(1)} collective-permute-done((bf16[192,3072]{1,0:T(8,128)(2,1)S(1)}, bf16[192,3072]{1,0:T(8,128)(2,1)S(1)}, u32[]{:S(2)}, u32[]{:S(2)}) %collective-permute-start.1) | collective-permute-done | bytes 1179680 | tf_op jit(solution)/shard_map/ppermute | solution.py:18
  43.3 16.5 %collective-permute-done.2 = bf16[192,3072]{1,0:T(8,128)(2,1)S(1)} collective-permute-done((bf16[192,3072]{1,0:T(8,128)(2,1)S(1)}, bf16[192,3072]{1,0:T(8,128)(2,1)S(1)}, u32[]{:S(2)}, u32[]{:S(2)}) %collective-permute-start.2) | collective-permute-done | bytes 1179680 | tf_op jit(solution)/shard_map/ppermute | solution.py:18
  59.8 16.5 %collective-permute-done.3 = bf16[192,3072]{1,0:T(8,128)(2,1)S(1)} collective-permute-done((bf16[192,3072]{1,0:T(8,128)(2,1)S(1)}, bf16[192,3072]{1,0:T(8,128)(2,1)S(1)}, u32[]{:S(2)}, u32[]{:S(2)}) %collective-permute-start.3) | collective-permute-done | bytes 1179680 | tf_op jit(solution)/shard_map/ppermute | solution.py:18
  77.3 16.5 %collective-permute-done.4 = bf16[192,3072]{1,0:T(8,128)(2,1)S(1)} collective-permute-done((bf16[192,3072]{1,0:T(8,128)(2,1)S(1)}, bf16[192,3072]{1,0:T(8,128)(2,1)S(1)}, u32[]{:S(2)}, u32[]{:S(2)}) %collective-permute-start.4) | collective-permute-done | bytes 1179680 | tf_op jit(solution)/shard_map/ppermute | solution.py:18
  94.9 16.6 %collective-permute-done.5 = bf16[192,3072]{1,0:T(8,128)(2,1)} collective-permute-done((bf16[192,3072]{1,0:T(8,128)(2,1)S(1)}, bf16[192,3072]{1,0:T(8,128)(2,1)}, u32[]{:S(2)}, u32[]{:S(2)}) %collective-permute-start.5) | collective-permute-done | bytes 1179680 | tf_op jit(solution)/shard_map/ppermute | solution.py:18
  111.5 16.8 %collective-permute-done.6 = bf16[192,3072]{1,0:T(8,128)(2,1)} collective-permute-done((bf16[192,3072]{1,0:T(8,128)(2,1)}, bf16[192,3072]{1,0:T(8,128)(2,1)}, u32[]{:S(2)}, u32[]{:S(2)}) %collective-permute-start.6) | collective-permute-done | bytes 1179680 | tf_op jit(solution)/shard_map/ppermute | solution.py:18
  128.4 1.3 constant_dynamic-update-slice_fusion.15
  129.7 1.3 constant_dynamic-update-slice_fusion.14
  132.7 1.3 constant_dynamic-update-slice_fusion.7
  134.0 1.3 constant_dynamic-update-slice_fusion.6
  136.1 6.5 %copy-done.5 = bf16[3072,3072]{1,0:T(8,128)(2,1)} copy-done((bf16[3072,3072]{1,0:T(8,128)(2,1)}, bf16[3072,3072]{1,0:T(8,128)(2,1)S(1)}, u32[]{:S(2)}) %copy-start.5) | copy-done | bytes 18874392
  142.5 5.2 %dynamic-slice_select_fusion = bf16[1536,1536]{1,0:T(8,128)(2,1)} fusion(bf16[3072,3072]{1,0:T(8,128)(2,1)S(1)} %constant_dynamic-update-slice_fusion, s32[]{:T(128)S(6)} %select_n.72, s32[]{:T(128)S(6)} %select_n.75, pred[]{:T(512)S(6)} %eq.23), kind=kLoop, calls=%fused_computation.4 | loop fusion | flops 2359296 | bytes 9437193 | tf_op jit(solution)/shard_map/jit(_where)/select_n | solution.py:31
  147.8 173.1 %all-reduce.2.cloned.1.call-done = bf16[1536,1536]{1,0:T(8,128)(2,1)} async-done(((bf16[1536,1536]{1,0:T(8,128)(2,1)}), bf16[1536,1536]{1,0:T(8,128)(2,1)}) %all-reduce.2.cloned.1.call-update) | async-done | bytes 4718608 | tf_op jit(solution)/shard_map/psum | solution.py:31
  320.9 20.5 %convolution_convert_fusion = bf16[1536,3072]{1,0:T(8,128)(2,1)} fusion(bf16[1536,1536]{1,0:T(8,128)(2,1)} %all-reduce.2.cloned.1.call-done, bf16[3072,1536]{1,0:T(8,128)(2,1)} %param.6), kind=kOutput, calls=%fused_computation.1 | convolution fusion | flops 14500233216 | bytes 23592960 | tf_op jit(solution)/shard_map/dot_general | solution.py:57
  342.7 2.0 scatter_fusion
  344.7 1.0 convert_element_type.31
  345.7 3.6 all-to-all-start
  349.4 68.1 %reduce-scatter.5.cloned.1.call-done = bf16[192,3072]{1,0:T(8,128)(2,1)} async-done(((bf16[1536,3072]{1,0:T(8,128)(2,1)}), bf16[192,3072]{1,0:T(8,128)(2,1)}) %reduce-scatter.5.cloned.1.call-update) | async-done | bytes 1179664 | tf_op jit(solution)/shard_map/reduce_scatter | solution.py:56
  417.4 1.6 select_convert_fusion
  419.0 4.5 fusion.2
  424.5 1.4 bitcast_convert_fusion
  425.9 19.5 %reduce-scatter.7.cloned.1.call-done = bf16[192,192]{1,0:T(8,128)(2,1)} async-done(((bf16[768,192]{1,0:T(8,128)(2,1)}), bf16[192,192]{1,0:T(8,128)(2,1)}) %reduce-scatter.7.cloned.1.call-update) | async-done | bytes 73744
  (55 shorter events, 9.5 us)
Async XLA Ops:
  7.2 313.8 %all-reduce.2.cloned.1.call-start = ((), (), s32[]{:S(2)}) async-start(), calls=%async_computation.3 | async-start | bytes 9437184 | tf_op jit(solution)/shard_map/psum | solution.py:31
  9.4 17.3 %collective-permute-start = (bf16[192,3072]{1,0:T(8,128)(2,1)S(1)}, bf16[192,3072]{1,0:T(8,128)(2,1)S(1)}, u32[]{:S(2)}, u32[]{:S(2)}) collective-permute-start(bf16[192,3072]{1,0:T(8,128)(2,1)S(1)} %broadcast_select_fusion), channel_id=1, source_target_pairs={{0,1},{1,2},{2,3},{3,4},{4,5},{5,6},{6,7},{7,0},{8,9},{9,10},{10,1... | collective-permute-start | bytes 3538952 | tf_op jit(solution)/shard_map/ppermute | solution.py:18
  26.7 16.5 %collective-permute-start.1 = (bf16[192,3072]{1,0:T(8,128)(2,1)S(1)}, bf16[192,3072]{1,0:T(8,128)(2,1)S(1)}, u32[]{:S(2)}, u32[]{:S(2)}) collective-permute-start(bf16[192,3072]{1,0:T(8,128)(2,1)S(1)} %collective-permute-done), channel_id=1, source_target_pairs={{0,1},{1,2},{2,3},{3,4},{4,5},{5,6},{6,7},{7,0},{8,9},{9,10},{10,1... | collective-permute-start | bytes 3538952 | tf_op jit(solution)/shard_map/ppermute | solution.py:18
  43.3 16.5 %collective-permute-start.2 = (bf16[192,3072]{1,0:T(8,128)(2,1)S(1)}, bf16[192,3072]{1,0:T(8,128)(2,1)S(1)}, u32[]{:S(2)}, u32[]{:S(2)}) collective-permute-start(bf16[192,3072]{1,0:T(8,128)(2,1)S(1)} %collective-permute-done.1), channel_id=1, source_target_pairs={{0,1},{1,2},{2,3},{3,4},{4,5},{5,6},{6,7},{7,0},{8,9},{9,10},{10,1... | collective-permute-start | bytes 3538952 | tf_op jit(solution)/shard_map/ppermute | solution.py:18
  59.8 16.5 %collective-permute-start.3 = (bf16[192,3072]{1,0:T(8,128)(2,1)S(1)}, bf16[192,3072]{1,0:T(8,128)(2,1)S(1)}, u32[]{:S(2)}, u32[]{:S(2)}) collective-permute-start(bf16[192,3072]{1,0:T(8,128)(2,1)S(1)} %collective-permute-done.2), channel_id=1, source_target_pairs={{0,1},{1,2},{2,3},{3,4},{4,5},{5,6},{6,7},{7,0},{8,9},{9,10},{10,1... | collective-permute-start | bytes 3538952 | tf_op jit(solution)/shard_map/ppermute | solution.py:18
  76.3 1.0 copy-start.1
  77.3 16.5 %collective-permute-start.4 = (bf16[192,3072]{1,0:T(8,128)(2,1)S(1)}, bf16[192,3072]{1,0:T(8,128)(2,1)S(1)}, u32[]{:S(2)}, u32[]{:S(2)}) collective-permute-start(bf16[192,3072]{1,0:T(8,128)(2,1)S(1)} %collective-permute-done.3), channel_id=1, source_target_pairs={{0,1},{1,2},{2,3},{3,4},{4,5},{5,6},{6,7},{7,0},{8,9},{9,10},{10,1... | collective-permute-start | bytes 3538952 | tf_op jit(solution)/shard_map/ppermute | solution.py:18
  93.9 1.0 copy-start.3
  94.9 16.6 %collective-permute-start.5 = (bf16[192,3072]{1,0:T(8,128)(2,1)S(1)}, bf16[192,3072]{1,0:T(8,128)(2,1)}, u32[]{:S(2)}, u32[]{:S(2)}) collective-permute-start(bf16[192,3072]{1,0:T(8,128)(2,1)S(1)} %collective-permute-done.4), channel_id=1, source_target_pairs={{0,1},{1,2},{2,3},{3,4},{4,5},{5,6},{6,7},{7,0},{8,9},{9,10},{10,1... | collective-permute-start | bytes 3538952 | tf_op jit(solution)/shard_map/ppermute | solution.py:18
  111.5 16.8 %collective-permute-start.6 = (bf16[192,3072]{1,0:T(8,128)(2,1)}, bf16[192,3072]{1,0:T(8,128)(2,1)}, u32[]{:S(2)}, u32[]{:S(2)}) collective-permute-start(bf16[192,3072]{1,0:T(8,128)(2,1)} %collective-permute-done.5), channel_id=1, source_target_pairs={{0,1},{1,2},{2,3},{3,4},{4,5},{5,6},{6,7},{7,0},{8,9},{9,10},{10,1... | collective-permute-start | bytes 3538952 | tf_op jit(solution)/shard_map/ppermute | solution.py:18
  111.5 19.5 %copy-start.4 = (bf16[192,3072]{1,0:T(8,128)(2,1)S(1)}, bf16[192,3072]{1,0:T(8,128)(2,1)}, u32[]{:S(2)}) copy-start(bf16[192,3072]{1,0:T(8,128)(2,1)} %copy-done.3) | copy-start | bytes 3538948
  111.5 19.6 %copy-start.2 = (bf16[192,3072]{1,0:T(8,128)(2,1)S(1)}, bf16[192,3072]{1,0:T(8,128)(2,1)}, u32[]{:S(2)}) copy-start(bf16[192,3072]{1,0:T(8,128)(2,1)} %copy-done.1) | copy-start | bytes 3538948
  131.2 1.3 copy-start
  136.1 6.5 %copy-start.5 = (bf16[3072,3072]{1,0:T(8,128)(2,1)}, bf16[3072,3072]{1,0:T(8,128)(2,1)S(1)}, u32[]{:S(2)}) copy-start(bf16[3072,3072]{1,0:T(8,128)(2,1)S(1)} %constant_dynamic-update-slice_fusion) | copy-start | bytes 56623108
  147.8 269.7 %reduce-scatter.5.cloned.1.call-start = ((), (), s32[]{:S(2)}) async-start(), calls=%async_computation.4 | async-start | bytes 10616832 | tf_op jit(solution)/shard_map/reduce_scatter | solution.py:56
  341.5 0.7 copy-start.9
  341.5 1.2 copy-start.7
  345.7 78.7 %all-to-all-start = ((bf16[32,3,32,128]{3,2,1,0:T(8,128)(2,1)}), bf16[32,3,32,128]{3,2,1,0:T(8,128)(2,1)S(1)}, u32[]{:S(2)}, u32[]{:S(2)}) async-start(bf16[32,3,32,128]{3,2,1,0:T(8,128)(2,1)} %bitcast.5), calls=%async_computation.1 | async-start | bytes 1572864 | tf_op jit(solution)/shard_map/all_to_all | solution.py:89
  349.3 96.2 %reduce-scatter.7.cloned.1.call-start = ((), (), s32[]{:S(2)}) async-start(), calls=%async_computation.5 | async-start | bytes 491520
  419.0 6.9 %copy-start.6 = (bf16[192,3072]{1,0:T(8,128)(2,1)}, bf16[192,3072]{1,0:T(8,128)(2,1)S(1)}, u32[]{:S(2)}) copy-start(bf16[192,3072]{1,0:T(8,128)(2,1)S(1)} %select_convert_fusion) | copy-start | bytes 3538948
  419.0 27.4 %copy-start.8 = (f32[192,192]{1,0:T(8,128)S(1)}, f32[192,192]{1,0:T(8,128)}, u32[]{:S(2)}) copy-start(f32[192,192]{1,0:T(8,128)} %param.8) | copy-start | bytes 442372
Sparse Core Ops, SparseCore 0:
  147.9 173.0 all-reduce.1
  341.6 75.7 reduce-scatter.4
  424.6 20.8 reduce-scatter.6
